TPU v7x, 32 devices: a whole 2x2x4 slice. The times are simulated.
32 devices in a mesh: rows: 4 (over z), cols: 2 (over x), slabs: 4 (over y, core).
Axes of the slice: x: 2, y: 2, z: 4, core: 2. Of those that a mesh axis runs over, the one named last changes fastest.
Arguments:
- tracer: float32 [16, 128, 256, 128], P('rows', 'cols', 'slabs'), may hold values from 0.2 to 1.8
- crowding: float32 [16, 128, 256, 128], P('rows', 'cols', 'slabs'), may hold values from 0.5 to 2
Outputs:
- column_sum: float32 [16, 128, 256, 128], P('rows', 'cols', 'slabs')
- tracer_end: float32 [16, 128, 256, 128], P('rows', 'cols', 'slabs')
All inputs are finite; a program needn't handle non-finite values.
Results may differ from a plain program's by a relative error of at most 0.00002.
Values sent between devices are 32-bit elements; how exact they have to be, the bound alone decides.
A program may use at most 320 MiB of HBM per device.

v0:
```python
import jax
import jax.numpy as jnp
from jax import lax
from jax.sharding import PartitionSpec as P

STEPS = 4


def padded_2(array, sides, width):
    for axis, dim in sides:
        count, length = (lax.axis_size(axis), array.shape[dim])
        up = [(i, (i + 1) % count) for i in range(count - 1)]
        down = [(j, i) for i, j in up]
        last = lax.slice_in_dim(array, length - width, length, axis=dim)
        initial = lax.slice_in_dim(array, 0, width, axis=dim)
        before = lax.ppermute(last, axis, up)
        after = lax.ppermute(initial, axis, down)
        array = jnp.concatenate([before, array, after], axis=dim)
    return array


def prefix(array, axis, combine, identity):
    count, place = (lax.axis_size(axis), lax.axis_index(axis))
    everything = lax.all_gather(array, axis)
    start = jnp.broadcast_to(jnp.asarray(identity, array.dtype), array.shape)

    def turn(k, before):
        reached = k < place
        new = combine(before, everything[k])
        return jnp.where(reached, new, before)

    return lax.fori_loop(0, count, turn, start)


def inner_cells(values, dims):
    for dim in dims:
        values = lax.slice_in_dim(values, 1, values.shape[dim] - 1, axis=dim)
    return values


def side_cells(values, dim, start, dims):
    others = [other for other in dims if other != dim]
    values = inner_cells(values, others)
    return lax.slice_in_dim(values, start, start + values.shape[dim] - 2, axis=dim)


def advance(padded, crowding):
    middle = inner_cells(padded, (0, 1, 2))
    lower = [side_cells(padded, dim, 0, (0, 1, 2)) for dim in (0, 1, 2)]
    upper = [side_cells(padded, dim, 2, (0, 1, 2)) for dim in (0, 1, 2)]
    spread = lower[0] + upper[0] + lower[1] + upper[1] + lower[2] + upper[2] - 6.0 * middle
    return middle + 0.1 * spread + 0.2 * middle * (1.0 - middle * crowding)


def body(tracer, crowding):
    for step in range(STEPS):
        padded = padded_2(tracer, (("rows", 0), ("cols", 1), ("slabs", 2)), 1)
        tracer = advance(padded, crowding)
    here = jnp.cumsum(tracer, axis=0)
    total = lax.slice_in_dim(here, here.shape[0] - 1, here.shape[0], axis=0)

    def add_pair(earlier_total, later_total):
        return earlier_total + later_total

    below = prefix(total, "rows", add_pair, jnp.zeros_like(total))
    column_sum = (here + below) / (tracer.shape[0] * lax.axis_size("rows"))
    return (column_sum, tracer)


def solution(mesh):
    placed = (P("rows", "cols", "slabs", None), P("rows", "cols", "slabs", None))
    return jax.shard_map(
        body,
        mesh=mesh,
        in_specs=placed,
        out_specs=(P("rows", "cols", "slabs", None), P("rows", "cols", "slabs", None)),
        check_vma=False,
    )
```

profile of v0, /device:TPU:24, one launch (start us, length us, event | category | flops | bytes accessed | tf_op | source)
XLA Modules:
  0.0 579.5 jit_solution(16554958363648953696)
XLA Ops:
  7.2 4.1 fusion.40
  12.8 5.9 %collective-permute-start.1 = (f32[1,64,64,128]{3,2,1,0:T(8,128)}, f32[1,64,64,128]{3,2,1,0:T(8,128)}, u32[]{:S(2)}, u32[]{:S(2)}) collective-permute-start(f32[1,64,64,128]{3,2,1,0:T(8,128)} %get-tuple-element.141), channel_id=1, source_target_pairs={{8,0},{16,8},{24,16},{9,1},{17,9},{25,17},{10,2},{18,10},{26,18},{... | collective-permute-start | bytes 6291464 | tf_op jit(solution)/shard_map/ppermute | solution.py:17
  18.6 42.1 %collective-permute-done = f32[1,64,64,128]{3,2,1,0:T(8,128)S(1)} collective-permute-done((f32[1,64,64,128]{3,2,1,0:T(8,128)S(1)}, f32[1,64,64,128]{3,2,1,0:T(8,128)S(1)}, u32[]{:S(2)}, u32[]{:S(2)}) %collective-permute-start) | collective-permute-done | bytes 2097184 | tf_op jit(solution)/shard_map/ppermute | solution.py:16
  72.7 4.3 collective-permute-done.3
  84.0 24.6 %fusion.31 = f32[4,64,64,128]{3,2,1,0:T(8,128)S(1)} fusion(f32[4,64,64,128]{3,2,1,0:T(8,128)} %param.4, f32[6,66,1,128]{3,2,1,0:T(1,128)S(1)} %copy.26, f32[6,1,64,128]{3,2,1,0:T(8,128)S(1)} %collective-permute-done.3, f32[6,64,64,128]{3,2,1,0:T(8,128)} %copy-done.3, f32[6,1,64,128]{3,2,1,0:T(8,128)S(1)} %collective-permute-done.2, ...), kind=kLoop, calls=%fused_computation.87 | loop fusion | flops 50331648 | bytes 42741760 | tf_op jit(solution)/shard_map/add | solution.py:52
  110.2 4.7 collective-permute-start.7
  114.9 41.0 %collective-permute-done.6 = f32[1,64,64,128]{3,2,1,0:T(8,128)S(1)} collective-permute-done((f32[1,64,64,128]{3,2,1,0:T(8,128)S(1)}, f32[1,64,64,128]{3,2,1,0:T(8,128)S(1)}, u32[]{:S(2)}, u32[]{:S(2)}) %collective-permute-start.6) | collective-permute-done | bytes 2097184 | tf_op jit(solution)/shard_map/ppermute | solution.py:16
  162.3 4.4 collective-permute-done.9
  167.0 3.9 collective-permute-start.10
  174.6 25.7 %fusion.22 = f32[4,64,64,128]{3,2,1,0:T(8,128)} fusion(f32[4,64,64,128]{3,2,1,0:T(8,128)} %copy-done.2, f32[6,66,1,128]{3,2,1,0:T(1,128)S(1)} %copy.30, f32[6,1,64,128]{3,2,1,0:T(8,128)S(1)} %collective-permute-done.9, f32[6,1,64,128]{3,2,1,0:T(8,128)S(1)} %collective-permute-done.8, f32[1,64,64,128]{3,2,1,0:T(8,128)S(1)} %collective-permute-done.7, ...), kind=kLoop, calls=%fused_computation.60 | loop fusion | flops 67108864 | bytes 30158848 | tf_op jit(solution)/shard_map/add | solution.py:52
  204.6 5.1 collective-permute-start.13
  209.7 40.7 %collective-permute-done.12 = f32[1,64,64,128]{3,2,1,0:T(8,128)S(1)} collective-permute-done((f32[1,64,64,128]{3,2,1,0:T(8,128)S(1)}, f32[1,64,64,128]{3,2,1,0:T(8,128)S(1)}, u32[]{:S(2)}, u32[]{:S(2)}) %collective-permute-start.12) | collective-permute-done | bytes 2097184 | tf_op jit(solution)/shard_map/ppermute | solution.py:16
  257.3 4.4 collective-permute-done.15
  262.0 3.8 collective-permute-start.16
  269.7 26.0 %fusion.13 = f32[4,64,64,128]{3,2,1,0:T(8,128)} fusion(f32[4,64,64,128]{3,2,1,0:T(8,128)} %fusion.22, f32[6,66,1,128]{3,2,1,0:T(1,128)S(1)} %copy.34, f32[6,1,64,128]{3,2,1,0:T(8,128)S(1)} %collective-permute-done.15, f32[6,1,64,128]{3,2,1,0:T(8,128)S(1)} %collective-permute-done.14, f32[1,64,64,128]{3,2,1,0:T(8,128)S(1)} %collective-permute-done.13, ...), kind=kLoop, calls=%fused_computation.33 | loop fusion | flops 67108864 | bytes 30158848 | tf_op jit(solution)/shard_map/add | solution.py:52
  299.9 5.1 collective-permute-start.19
  305.1 40.7 %collective-permute-done.18 = f32[1,64,64,128]{3,2,1,0:T(8,128)S(1)} collective-permute-done((f32[1,64,64,128]{3,2,1,0:T(8,128)S(1)}, f32[1,64,64,128]{3,2,1,0:T(8,128)S(1)}, u32[]{:S(2)}, u32[]{:S(2)}) %collective-permute-start.18) | collective-permute-done | bytes 2097184 | tf_op jit(solution)/shard_map/ppermute | solution.py:16
  352.3 4.4 collective-permute-done.21
  357.0 4.0 collective-permute-start.22
  365.0 25.7 %fusion.4 = f32[4,64,64,128]{3,2,1,0:T(8,128)} fusion(f32[4,64,64,128]{3,2,1,0:T(8,128)} %fusion.13, f32[6,66,1,128]{3,2,1,0:T(1,128)S(1)} %copy.38, f32[6,1,64,128]{3,2,1,0:T(8,128)S(1)} %collective-permute-done.21, f32[6,1,64,128]{3,2,1,0:T(8,128)S(1)} %collective-permute-done.20, f32[1,64,64,128]{3,2,1,0:T(8,128)S(1)} %collective-permute-done.19, ...), kind=kLoop, calls=%fused_computation.6 | loop fusion | flops 67108864 | bytes 30158848 | tf_op jit(solution)/shard_map/add | solution.py:52
  390.8 8.7 %fusion.41 = f32[4,64,64,128]{3,2,1,0:T(8,128)} fusion(f32[4,64,64,128]{3,2,1,0:T(8,128)} %fusion.4), kind=kOutput, calls=%fused_computation.137 | output fusion | flops 6291456 | bytes 16777216 | tf_op jit(solution)/shard_map/jit(cumsum)/reduce_window_sum | solution.py:59
  402.7 151.8 %all-gather.3.cloned.1.call-done = f32[4,64,64,128]{3,2,1,0:T(8,128)} async-done(((f32[1,64,64,128]{3,2,1,0:T(8,128)}), f32[4,64,64,128]{3,2,1,0:T(8,128)}) %all-gather.3.cloned.1.call-update) | async-done | bytes 8388624 | tf_op jit(solution)/shard_map/all_gather | solution.py:24
  554.5 9.3 %while.14 = (s32[]{:T(128)}, f32[1,64,64,128]{3,2,1,0:T(8,128)S(1)}, s32[]{:T(128)}, f32[4,1,64,64,128]{4,3,2,1,0:T(8,128)}, s32[]{:T(128)}, /*index=5*/s32[]{:T(128)}) while((s32[]{:T(128)}, f32[1,64,64,128]{3,2,1,0:T(8,128)S(1)}, s32[]{:T(128)}, f32[4,1,64,64,128]{4,3,2,1,0:T(8,128)}, s32[]{:T(128)}, /*index=5*/s32[]{:T(128)}) %tuple.57), condition=%wide.region_2.3_spmd.clone, body=%wide.region_1.2_spmd.clone.sunk | while | flops 1572868 | bytes 6291549 | solution.py:32
  563.8 8.8 %add_multiply_fusion = f32[4,64,64,128]{3,2,1,0:T(8,128)} fusion(f32[4,64,64,128]{3,2,1,0:T(8,128)} %fusion.41, f32[64,64,128]{2,1,0:T(8,128)S(1)} %bitcast.9), kind=kLoop, calls=%fused_computation.101 | loop fusion | flops 4194304 | bytes 18874368 | tf_op jit(solution)/shard_map/div | solution.py:66
  (85 shorter events, 74.8 us)
Async XLA Ops:
  7.2 547.3 %all-gather.3.cloned.1.call-start = ((), (), s32[]{:S(2)}) async-start(), calls=%async_computation | async-start | bytes 10485760 | tf_op jit(solution)/shard_map/all_gather | solution.py:24
  11.4 49.4 %collective-permute-start = (f32[1,64,64,128]{3,2,1,0:T(8,128)S(1)}, f32[1,64,64,128]{3,2,1,0:T(8,128)S(1)}, u32[]{:S(2)}, u32[]{:S(2)}) collective-permute-start(f32[1,64,64,128]{3,2,1,0:T(8,128)S(1)} %get-tuple-element.142), channel_id=1, source_target_pairs={{0,8},{8,16},{16,24},{1,9},{9,17},{17,25},{2,10},{10,18},{18,26},{... | collective-permute-start | bytes 6291464 | tf_op jit(solution)/shard_map/ppermute | solution.py:16
  12.8 51.2 %collective-permute-start.1 = (f32[1,64,64,128]{3,2,1,0:T(8,128)}, f32[1,64,64,128]{3,2,1,0:T(8,128)}, u32[]{:S(2)}, u32[]{:S(2)}) collective-permute-start(f32[1,64,64,128]{3,2,1,0:T(8,128)} %get-tuple-element.141), channel_id=1, source_target_pairs={{8,0},{16,8},{24,16},{9,1},{17,9},{25,17},{10,2},{18,10},{26,18},{... | collective-permute-start | bytes 6291464 | tf_op jit(solution)/shard_map/ppermute | solution.py:17
  65.8 7.0 %collective-permute-start.2 = (f32[6,1,64,128]{3,2,1,0:T(8,128)S(1)}, f32[6,1,64,128]{3,2,1,0:T(8,128)S(1)}, u32[]{:S(2)}, u32[]{:S(2)}) collective-permute-start(f32[6,1,64,128]{3,2,1,0:T(8,128)S(1)} %get-tuple-element.133), channel_id=1, source_target_pairs={{0,4},{1,5},{2,6},{3,7},{8,12},{9,13},{10,14},{11,15},{16,20},{17,... | collective-permute-start | bytes 589832 | tf_op jit(solution)/shard_map/ppermute | solution.py:16
  69.5 7.6 %collective-permute-start.3 = (f32[6,1,64,128]{3,2,1,0:T(8,128)S(1)}, f32[6,1,64,128]{3,2,1,0:T(8,128)S(1)}, u32[]{:S(2)}, u32[]{:S(2)}) collective-permute-start(f32[6,1,64,128]{3,2,1,0:T(8,128)S(1)} %get-tuple-element.134), channel_id=1, source_target_pairs={{4,0},{5,1},{6,2},{7,3},{12,8},{13,9},{14,10},{15,11},{20,16},{21,... | collective-permute-start | bytes 589832 | tf_op jit(solution)/shard_map/ppermute | solution.py:17
  78.7 5.1 collective-permute-start.5
  108.9 47.0 %collective-permute-start.6 = (f32[1,64,64,128]{3,2,1,0:T(8,128)S(1)}, f32[1,64,64,128]{3,2,1,0:T(8,128)S(1)}, u32[]{:S(2)}, u32[]{:S(2)}) collective-permute-start(f32[1,64,64,128]{3,2,1,0:T(8,128)S(1)} %get-tuple-element.139), channel_id=1, source_target_pairs={{0,8},{8,16},{16,24},{1,9},{9,17},{17,25},{2,10},{10,18},{18,26},{... | collective-permute-start | bytes 6291464 | tf_op jit(solution)/shard_map/ppermute | solution.py:16
  110.2 47.4 %collective-permute-start.7 = (f32[1,64,64,128]{3,2,1,0:T(8,128)S(1)}, f32[1,64,64,128]{3,2,1,0:T(8,128)S(1)}, u32[]{:S(2)}, u32[]{:S(2)}) collective-permute-start(f32[1,64,64,128]{3,2,1,0:T(8,128)S(1)} %get-tuple-element.140), channel_id=1, source_target_pairs={{8,0},{16,8},{24,16},{9,1},{17,9},{25,17},{10,2},{18,10},{26,18},{... | collective-permute-start | bytes 6291464 | tf_op jit(solution)/shard_map/ppermute | solution.py:17
  157.7 4.6 collective-permute-start.8
  159.2 7.6 %collective-permute-start.9 = (f32[6,1,64,128]{3,2,1,0:T(8,128)S(1)}, f32[6,1,64,128]{3,2,1,0:T(8,128)S(1)}, u32[]{:S(2)}, u32[]{:S(2)}) collective-permute-start(f32[6,1,64,128]{3,2,1,0:T(8,128)S(1)} %get-tuple-element.132), channel_id=1, source_target_pairs={{4,0},{5,1},{6,2},{7,3},{12,8},{13,9},{14,10},{15,11},{20,16},{21,... | collective-permute-start | bytes 589832 | tf_op jit(solution)/shard_map/ppermute | solution.py:17
  167.0 5.4 collective-permute-start.10
  170.9 3.5 collective-permute-start.11
  203.0 47.4 %collective-permute-start.12 = (f32[1,64,64,128]{3,2,1,0:T(8,128)S(1)}, f32[1,64,64,128]{3,2,1,0:T(8,128)S(1)}, u32[]{:S(2)}, u32[]{:S(2)}) collective-permute-start(f32[1,64,64,128]{3,2,1,0:T(8,128)S(1)} %get-tuple-element.137), channel_id=1, source_target_pairs={{0,8},{8,16},{16,24},{1,9},{9,17},{17,25},{2,10},{10,18},{18,26},{... | collective-permute-start | bytes 6291464 | tf_op jit(solution)/shard_map/ppermute | solution.py:16
  204.6 47.6 %collective-permute-start.13 = (f32[1,64,64,128]{3,2,1,0:T(8,128)S(1)}, f32[1,64,64,128]{3,2,1,0:T(8,128)S(1)}, u32[]{:S(2)}, u32[]{:S(2)}) collective-permute-start(f32[1,64,64,128]{3,2,1,0:T(8,128)S(1)} %get-tuple-element.138), channel_id=1, source_target_pairs={{8,0},{16,8},{24,16},{9,1},{17,9},{25,17},{10,2},{18,10},{26,18},{... | collective-permute-start | bytes 6291464 | tf_op jit(solution)/shard_map/ppermute | solution.py:17
  252.2 5.0 collective-permute-start.14
  254.1 7.6 %collective-permute-start.15 = (f32[6,1,64,128]{3,2,1,0:T(8,128)S(1)}, f32[6,1,64,128]{3,2,1,0:T(8,128)S(1)}, u32[]{:S(2)}, u32[]{:S(2)}) collective-permute-start(f32[6,1,64,128]{3,2,1,0:T(8,128)S(1)} %get-tuple-element.130), channel_id=1, source_target_pairs={{4,0},{5,1},{6,2},{7,3},{12,8},{13,9},{14,10},{15,11},{20,16},{21,... | collective-permute-start | bytes 589832 | tf_op jit(solution)/shard_map/ppermute | solution.py:17
  262.0 5.2 collective-permute-start.16
  265.9 3.6 collective-permute-start.17
  298.4 47.4 %collective-permute-start.18 = (f32[1,64,64,128]{3,2,1,0:T(8,128)S(1)}, f32[1,64,64,128]{3,2,1,0:T(8,128)S(1)}, u32[]{:S(2)}, u32[]{:S(2)}) collective-permute-start(f32[1,64,64,128]{3,2,1,0:T(8,128)S(1)} %get-tuple-element.135), channel_id=1, source_target_pairs={{0,8},{8,16},{16,24},{1,9},{9,17},{17,25},{2,10},{10,18},{18,26},{... | collective-permute-start | bytes 6291464 | tf_op jit(solution)/shard_map/ppermute | solution.py:16
  299.9 47.6 %collective-permute-start.19 = (f32[1,64,64,128]{3,2,1,0:T(8,128)S(1)}, f32[1,64,64,128]{3,2,1,0:T(8,128)S(1)}, u32[]{:S(2)}, u32[]{:S(2)}) collective-permute-start(f32[1,64,64,128]{3,2,1,0:T(8,128)S(1)} %get-tuple-element.136), channel_id=1, source_target_pairs={{8,0},{16,8},{24,16},{9,1},{17,9},{25,17},{10,2},{18,10},{26,18},{... | collective-permute-start | bytes 6291464 | tf_op jit(solution)/shard_map/ppermute | solution.py:17
  347.6 4.7 collective-permute-start.20
  349.1 7.6 %collective-permute-start.21 = (f32[6,1,64,128]{3,2,1,0:T(8,128)S(1)}, f32[6,1,64,128]{3,2,1,0:T(8,128)S(1)}, u32[]{:S(2)}, u32[]{:S(2)}) collective-permute-start(f32[6,1,64,128]{3,2,1,0:T(8,128)S(1)} %get-tuple-element.128), channel_id=1, source_target_pairs={{4,0},{5,1},{6,2},{7,3},{12,8},{13,9},{14,10},{15,11},{20,16},{21,... | collective-permute-start | bytes 589832 | tf_op jit(solution)/shard_map/ppermute | solution.py:17
  357.0 5.6 collective-permute-start.22
  361.1 3.7 collective-permute-start.23
  (8 other events, 257.3 us)
Sparse Core Ops, SparseCore 0:
  402.8 151.6 all-gather.2
where the time goes:
time: 585 us; the launch traced here: 579 us
  waiting for transfers between devices  356 us (61%)
  other arithmetic  130 us (22%)
  starting transfers between devices  59 us (10%)
  local copies, waits for them, and re-layouts  19.8 us (3%)
  between operations  14.5 us (2%)
    ppermute x12, waiting for transfers between devices, padded_2(): before = lax.ppermute(last, axis, up)  172 us
    all_gather x1, waiting for transfers between devices, prefix(): everything = lax.all_gather(array, axis)  152 us
    add x4, other arithmetic, advance(): return middle + 0.1 * spread + 0.2 * middle * (1.0 - middle * crowding)  102 us
    ppermute x12, waiting for transfers between devices, padded_2(): after = lax.ppermute(initial, axis, down)  32.2 us
    ppermute x12, starting transfers between devices, padded_2(): after = lax.ppermute(initial, axis, down)  31.6 us
    ppermute x12, starting transfers between devices, padded_2(): before = lax.ppermute(last, axis, up)  27.4 us
  transfers between devices with their start and end apart: 25, of which 20 were waited for; matrix products, arithmetic and copies ran while one was open for 0% of the time, Pallas kernels for 0%

commit v1 on v0

v1 whole, which is shorter than its diff:
```python
import functools
import math

import jax
import jax.numpy as jnp
from jax import lax
from jax.experimental import pallas as pl
from jax.experimental.pallas import tpu as pltpu
from jax.sharding import PartitionSpec as P

STEPS = 4
CHUNK = 4
MESH = pl.DeviceIdType.MESH


def evolve(
    sizes, chunk, tracer, crowding, end, below,
    field, crowd, edge_out, edge_in, prefix_in, prefix_out,
    row_send, row_recv, col_send, col_recv, slab_send, slab_recv, pre_send, pre_recv, local_sem,
):
    depth, width, length, _ = tracer.shape
    chunks = width // chunk
    place = {axis: lax.axis_index(axis) for axis in sizes}
    has = {axis: (place[axis] > 0, place[axis] < sizes[axis] - 1) for axis in sizes}

    def other(axis, side):
        step = 1 if side else sizes[axis] - 1
        return {axis: lax.rem(place[axis] + step, sizes[axis])}

    def rows_of(c):
        return pl.ds(c * chunk, chunk), pl.ds(1 + c * chunk, chunk)

    def row_copy(step, side, c):
        slot = step % 2
        inner, padded = rows_of(c)
        if step == 0:
            source = tracer.at[depth - 1 if side else 0, inner]
        else:
            source = field.at[slot, depth if side else 1, padded]
        return pltpu.make_async_remote_copy(
            source, field.at[slot, 0 if side else depth + 1, padded],
            row_send.at[slot, side, c], row_recv.at[slot, side, c],
            device_id=other("rows", side), device_id_type=MESH,
        )

    def col_copy(step, side):
        slot = step % 2
        planes = pl.ds(1, depth)
        if step == 0:
            source = tracer.at[:, width - 1 if side else 0]
        else:
            source = field.at[slot, planes, width if side else 1]
        return pltpu.make_async_remote_copy(
            source, field.at[slot, planes, 0 if side else width + 1],
            col_send.at[slot, side], col_recv.at[slot, side],
            device_id=other("cols", side), device_id_type=MESH,
        )

    def slab_copy(step, side):
        slot = step % 2
        return pltpu.make_async_remote_copy(
            edge_out.at[slot, side], edge_in.at[slot, side],
            slab_send.at[slot, side], slab_recv.at[slot, side],
            device_id=other("slabs", side), device_id_type=MESH,
        )

    def prefix_copy(c):
        inner, _ = rows_of(c)
        return pltpu.make_async_remote_copy(
            prefix_out.at[inner], prefix_in.at[inner], pre_send.at[c], pre_recv.at[c],
            device_id=other("rows", 1), device_id_type=MESH,
        )

    load_field = pltpu.make_async_copy(tracer, field.at[0, pl.ds(1, depth), pl.ds(1, width)], local_sem.at[0])
    load_crowd = pltpu.make_async_copy(crowding, crowd, local_sem.at[1])
    load_field.start()
    load_crowd.start()

    barrier = pltpu.get_barrier_semaphore()
    greeted = 0
    for axis in sizes:
        for side in (0, 1):
            greeted += has[axis][side].astype(jnp.int32)

            @pl.when(has[axis][side])
            def _():
                pl.semaphore_signal(barrier, inc=1, device_id=other(axis, side), device_id_type=MESH)

    pl.semaphore_wait(barrier, greeted)

    def each_chunk(turn):
        lax.fori_loop(0, chunks, lambda c, carry: (turn(c), carry)[1], 0)

    def start_rows(c):
        for side in (0, 1):
            @pl.when(has["rows"][side])
            def _():
                row_copy(0, side, c).start()

    each_chunk(start_rows)
    for side in (0, 1):
        @pl.when(has["cols"][side])
        def _():
            col_copy(0, side).start()

    for side in (0, 1):
        @pl.when(jnp.logical_not(has["rows"][side]))
        def _():
            def clear(c):
                for slot in (0, 1):
                    field[slot, depth + 1 if side else 0, pl.ds(1 + c * chunk, chunk)] = jnp.zeros(
                        (chunk,) + field.shape[3:], field.dtype)
            each_chunk(clear)

        @pl.when(jnp.logical_not(has["cols"][side]))
        def _():
            for slot in (0, 1):
                for plane in range(depth):
                    field[slot, 1 + plane, width + 1 if side else 0] = jnp.zeros(field.shape[3:], field.dtype)

        @pl.when(jnp.logical_not(has["slabs"][side]))
        def _():
            for slot in (0, 1):
                edge_in[slot, 1 - side] = jnp.zeros(edge_in.shape[2:], field.dtype)

    @pl.when(jnp.logical_not(has["rows"][0]))
    def _():
        def clear(c):
            prefix_in[pl.ds(c * chunk, chunk)] = jnp.zeros((chunk,) + prefix_in.shape[1:], field.dtype)
        each_chunk(clear)

    load_field.wait()

    def pack(x, carry):
        for plane in range(depth):
            edge_out[0, 0, plane, pl.ds(x, 1), :] = field[0, 1 + plane, 1 + x, 0:1, :]
            edge_out[0, 1, plane, pl.ds(x, 1), :] = field[0, 1 + plane, 1 + x, length - 1:length, :]
        return carry

    lax.fori_loop(0, width, pack, 0)
    for side in (0, 1):
        @pl.when(has["slabs"][side])
        def _():
            slab_copy(0, side).start()

    load_crowd.wait()

    for step in range(STEPS):
        now, later = step % 2, (step + 1) % 2
        last = step == STEPS - 1
        for side in (0, 1):
            for axis, copy in (("cols", col_copy), ("slabs", slab_copy)):
                if step >= 1:
                    @pl.when(has[axis][side])
                    def _():
                        copy(step - 1, side).wait_send()

                @pl.when(has[axis][1 - side])
                def _():
                    copy(step, side).wait_recv()

        def turn(c):
            for side in (0, 1):
                if step >= 1:
                    @pl.when(has["rows"][side])
                    def _():
                        row_copy(step - 1, side, c).wait_send()

                @pl.when(has["rows"][1 - side])
                def _():
                    row_copy(step, side, c).wait_recv()

            def line(i, carry):
                x = c * chunk + i
                spot = lax.broadcasted_iota(jnp.int32, (length, field.shape[4]), 0)
                column = [field[now, plane, 1 + x] for plane in range(depth + 2)]
                total = None
                for plane in range(depth):
                    middle = column[plane + 1]
                    ahead = edge_in[now, 1, plane, pl.ds(x, 1), :]
                    behind = edge_in[now, 0, plane, pl.ds(x, 1), :]
                    lower = jnp.where(spot == 0, ahead, pltpu.roll(middle, 1, 0))
                    upper = jnp.where(spot == length - 1, behind, pltpu.roll(middle, length - 1, 0))
                    spread = (
                        column[plane] + column[plane + 2]
                        + field[now, plane + 1, x] + field[now, plane + 1, x + 2]
                        + lower + upper - 6.0 * middle
                    )
                    new = middle + 0.1 * spread + 0.2 * middle * (1.0 - middle * crowd[plane, x])
                    field[later, plane + 1, 1 + x] = new
                    if last:
                        total = new if total is None else total + new
                    else:
                        edge_out[later, 0, plane, pl.ds(x, 1), :] = new[0:1, :]
                        edge_out[later, 1, plane, pl.ds(x, 1), :] = new[length - 1:length, :]
                if last:
                    prefix_out[x] = total
                return carry

            lax.fori_loop(0, chunk, line, 0)
            if last:
                @pl.when(jnp.logical_and(jnp.logical_not(has["rows"][0]), has["rows"][1]))
                def _():
                    prefix_copy(c).start()
            else:
                for side in (0, 1):
                    @pl.when(has["rows"][side])
                    def _():
                        row_copy(step + 1, side, c).start()

        each_chunk(turn)
        if not last:
            for side in (0, 1):
                for axis, copy in (("cols", col_copy), ("slabs", slab_copy)):
                    @pl.when(has[axis][side])
                    def _():
                        copy(step + 1, side).start()

    final = STEPS % 2
    store_end = pltpu.make_async_copy(field.at[final, pl.ds(1, depth), pl.ds(1, width)], end, local_sem.at[0])
    store_end.start()

    @pl.when(has["rows"][0])
    def _():
        def forward(c):
            prefix_copy(c).wait_recv()

            @pl.when(has["rows"][1])
            def _():
                inner = pl.ds(c * chunk, chunk)
                prefix_out[inner] = prefix_out[inner] + prefix_in[inner]
                prefix_copy(c).start()
        each_chunk(forward)

    store_below = pltpu.make_async_copy(prefix_in, below, local_sem.at[1])
    store_below.start()

    def drain(c):
        for side in (0, 1):
            @pl.when(has["rows"][side])
            def _():
                row_copy(STEPS - 1, side, c).wait_send()

        @pl.when(has["rows"][1])
        def _():
            prefix_copy(c).wait_send()

    each_chunk(drain)
    for side in (0, 1):
        for axis, copy in (("cols", col_copy), ("slabs", slab_copy)):
            @pl.when(has[axis][side])
            def _():
                copy(STEPS - 1, side).wait_send()
    store_end.wait()
    store_below.wait()


def finish(count, end, below, column_sum, tracer_end):
    running = below[...]
    for plane in range(end.shape[0]):
        value = end[plane]
        running = running + value
        tracer_end[plane] = value
        column_sum[plane] = running / count


def body(sizes, tracer, crowding):
    depth, width, length, levels = tracer.shape
    kind = tracer.dtype
    chunk = math.gcd(width, CHUNK)
    chunks = width // chunk
    anywhere = pl.BlockSpec(memory_space=pl.ANY)
    dma = pltpu.SemaphoreType.DMA
    end, below = pl.pallas_call(
        functools.partial(evolve, sizes, chunk),
        out_shape=(
            jax.ShapeDtypeStruct(tracer.shape, kind),
            jax.ShapeDtypeStruct(tracer.shape[1:], kind),
        ),
        in_specs=[anywhere, anywhere],
        out_specs=(anywhere, anywhere),
        scratch_shapes=[
            pltpu.VMEM((2, depth + 2, width + 2, length, levels), kind),
            pltpu.VMEM(tracer.shape, kind),
            pltpu.VMEM((2, 2, depth, width, levels), kind),
            pltpu.VMEM((2, 2, depth, width, levels), kind),
            pltpu.VMEM(tracer.shape[1:], kind),
            pltpu.VMEM(tracer.shape[1:], kind),
            dma((2, 2, chunks)), dma((2, 2, chunks)),
            dma((2, 2)), dma((2, 2)),
            dma((2, 2)), dma((2, 2)),
            dma((chunks,)), dma((chunks,)),
            dma((2,)),
        ],
        compiler_params=pltpu.CompilerParams(
            collective_id=0, has_side_effects=True, vmem_limit_bytes=60 * 1024 * 1024
        ),
        name="evolve",
    )(tracer, crowding)

    block = math.gcd(width, 8)
    whole = pl.BlockSpec((depth, block, length, levels), lambda i: (0, i, 0, 0))
    plane = pl.BlockSpec((block, length, levels), lambda i: (i, 0, 0))
    return pl.pallas_call(
        functools.partial(finish, depth * sizes["rows"]),
        grid=(width // block,),
        out_shape=(jax.ShapeDtypeStruct(tracer.shape, kind),) * 2,
        in_specs=[whole, plane],
        out_specs=(whole, whole),
        name="finish",
    )(end, below)


def solution(mesh):
    sizes = {axis: mesh.shape[axis] for axis in ("rows", "cols", "slabs")}
    placed = P("rows", "cols", "slabs", None)
    return jax.shard_map(
        functools.partial(body, sizes),
        mesh=mesh,
        in_specs=(placed, placed),
        out_specs=(placed, placed),
        check_vma=False,
    )
```

time: 585 us -> 251 us (0.43)
  waiting for transfers between devices: 356 us -> 0 us
  Pallas kernels: 0 us -> 250 us
  other arithmetic: 130 us -> 0 us
  starting transfers between devices: 59 us -> 0 us
  local copies, waits for them, and re-layouts: 19.8 us -> 0 us
  between operations: 14.5 us -> 0.64 us
    pallas_call x0 -> x2, Pallas kernels: none -> 250 us  [the longest x1 239 us: body(): pl.pallas_call(functools.partial(evolve, sizes, chunk), out_shape=(jax.Sh...]
    ppermute x24 -> x0, waiting for transfers between devices: 204 us -> none  [the longest x12 172 us: padded_2(): before = lax.ppermute(last, axis, up)]
    all_gather x1 -> x0, waiting for transfers between devices: 152 us -> none  [prefix(): everything = lax.all_gather(array, axis)]
    add x4 -> x0, other arithmetic: 102 us -> none  [advance(): return middle + 0.1 * spread + 0.2 * middle * (1.0 - middle * crowding)]
    ppermute x24 -> x0, starting transfers between devices: 59 us -> none  [the longest x12 31.6 us: padded_2(): after = lax.ppermute(initial, axis, down)]
    slice x14 -> x0, local copies, waits for them, and re-layouts: 13.2 us -> none  [the longest x8 5.78 us: padded_2(): last = lax.slice_in_dim(array, length - width, length, axis=dim)]
    select_n x4 -> x0, other arithmetic: 9.24 us -> none  [turn(): return jnp.where(reached, new, before)]
    div x1 -> x0, other arithmetic: 8.78 us -> none  [body(): column_sum = (here + below) / (tracer.shape[0] * lax.axis_size('rows'))]
  transfers between devices with their start and end apart: 25 -> 0, of which waited for: 20 -> 0; matrix products, arithmetic and copies ran while one was open for 0% -> 0% of each run, Pallas kernels for 0% -> 0%
where the time goes in v1:
time: 251 us
  Pallas kernels  250 us (100%)
    pallas_call x1, Pallas kernels, body(): pl.pallas_call(functools.partial(evolve, sizes, chunk), out_shape=(jax.Sh...  239 us
    pallas_call x1, Pallas kernels, body(): pl.pallas_call(functools.partial(finish, depth * sizes['rows']), grid=(wi...  11.3 us

profile of v1, /device:TPU:24, one launch (start us, length us, event | category | flops | bytes accessed | tf_op | source)
XLA Modules:
  0.0 250.6 jit_solution(3360390252518462424)
XLA Ops:
  0.6 238.7 %evolve.1 = (f32[4,64,64,128]{3,2,1,0:T(8,128)}, f32[64,64,128]{2,1,0:T(8,128)}) custom-call(f32[4,64,64,128]{3,2,1,0:T(8,128)} %tracer.1, f32[4,64,64,128]{3,2,1,0:T(8,128)} %crowding.1), custom_call_target="tpu_custom_call" | custom-call | tf_op jit(solution)/shard_map/evolve/pallas_call | solution.py:274
  239.3 11.3 %finish.1 = (f32[4,64,64,128]{3,2,1,0:T(8,128)}, f32[4,64,64,128]{3,2,1,0:T(8,128)}) custom-call(f32[4,64,64,128]{3,2,1,0:T(8,128)} %get-tuple-element.4.end, f32[64,64,128]{2,1,0:T(8,128)} %get-tuple-element.5.below), custom_call_target="tpu_custom_call" | custom-call | tf_op jit(solution)/shard_map/finish/pallas_call | solution.py:304

commit v2 on v1

--- a/solution.py
+++ b/solution.py
@@ -10,16 +10,17 @@
 
 STEPS = 4
 CHUNK = 4
+PIECE = 1
 MESH = pl.DeviceIdType.MESH
 
 
 def evolve(
-    sizes, chunk, tracer, crowding, end, below,
-    field, crowd, edge_out, edge_in, prefix_in, prefix_out,
+    sizes, chunk, piece, tracer, crowding, end, below,
+    field, crowd, edge_out, edge_in, prefix_out,
     row_send, row_recv, col_send, col_recv, slab_send, slab_recv, pre_send, pre_recv, local_sem,
 ):
     depth, width, length, _ = tracer.shape
-    chunks = width // chunk
+    chunks, pieces = width // chunk, width // piece
     place = {axis: lax.axis_index(axis) for axis in sizes}
     has = {axis: (place[axis] > 0, place[axis] < sizes[axis] - 1) for axis in sizes}
 
@@ -65,9 +66,9 @@
         )
 
     def prefix_copy(c):
-        inner, _ = rows_of(c)
+        inner = pl.ds(c * piece, piece)
         return pltpu.make_async_remote_copy(
-            prefix_out.at[inner], prefix_in.at[inner], pre_send.at[c], pre_recv.at[c],
+            prefix_out.at[inner], below.at[inner], pre_send.at[c], pre_recv.at[c],
             device_id=other("rows", 1), device_id_type=MESH,
         )
 
@@ -88,8 +89,8 @@
 
     pl.semaphore_wait(barrier, greeted)
 
-    def each_chunk(turn):
-        lax.fori_loop(0, chunks, lambda c, carry: (turn(c), carry)[1], 0)
+    def each(count, turn):
+        lax.fori_loop(0, count, lambda c, carry: (turn(c), carry)[1], 0)
 
     def start_rows(c):
         for side in (0, 1):
@@ -97,7 +98,7 @@
             def _():
                 row_copy(0, side, c).start()
 
-    each_chunk(start_rows)
+    each(chunks, start_rows)
     for side in (0, 1):
         @pl.when(has["cols"][side])
         def _():
@@ -110,7 +111,7 @@
                 for slot in (0, 1):
                     field[slot, depth + 1 if side else 0, pl.ds(1 + c * chunk, chunk)] = jnp.zeros(
                         (chunk,) + field.shape[3:], field.dtype)
-            each_chunk(clear)
+            each(chunks, clear)
 
         @pl.when(jnp.logical_not(has["cols"][side]))
         def _():
@@ -126,8 +127,8 @@
     @pl.when(jnp.logical_not(has["rows"][0]))
     def _():
         def clear(c):
-            prefix_in[pl.ds(c * chunk, chunk)] = jnp.zeros((chunk,) + prefix_in.shape[1:], field.dtype)
-        each_chunk(clear)
+            below[pl.ds(c * chunk, chunk)] = jnp.zeros((chunk,) + below.shape[1:], field.dtype)
+        each(chunks, clear)
 
     load_field.wait()
 
@@ -187,10 +188,11 @@
                         + lower + upper - 6.0 * middle
                     )
                     new = middle + 0.1 * spread + 0.2 * middle * (1.0 - middle * crowd[plane, x])
-                    field[later, plane + 1, 1 + x] = new
                     if last:
+                        end[plane, x] = new
                         total = new if total is None else total + new
                     else:
+                        field[later, plane + 1, 1 + x] = new
                         edge_out[later, 0, plane, pl.ds(x, 1), :] = new[0:1, :]
                         edge_out[later, 1, plane, pl.ds(x, 1), :] = new[length - 1:length, :]
                 if last:
@@ -201,14 +203,15 @@
             if last:
                 @pl.when(jnp.logical_and(jnp.logical_not(has["rows"][0]), has["rows"][1]))
                 def _():
-                    prefix_copy(c).start()
+                    for k in range(chunk // piece):
+                        prefix_copy(c * (chunk // piece) + k).start()
             else:
                 for side in (0, 1):
                     @pl.when(has["rows"][side])
                     def _():
                         row_copy(step + 1, side, c).start()
 
-        each_chunk(turn)
+        each(chunks, turn)
         if not last:
             for side in (0, 1):
                 for axis, copy in (("cols", col_copy), ("slabs", slab_copy)):
@@ -216,10 +219,6 @@
                     def _():
                         copy(step + 1, side).start()
 
-    final = STEPS % 2
-    store_end = pltpu.make_async_copy(field.at[final, pl.ds(1, depth), pl.ds(1, width)], end, local_sem.at[0])
-    store_end.start()
-
     @pl.when(has["rows"][0])
     def _():
         def forward(c):
@@ -227,13 +226,10 @@
 
             @pl.when(has["rows"][1])
             def _():
-                inner = pl.ds(c * chunk, chunk)
-                prefix_out[inner] = prefix_out[inner] + prefix_in[inner]
+                inner = pl.ds(c * piece, piece)
+                prefix_out[inner] = prefix_out[inner] + below[inner]
                 prefix_copy(c).start()
-        each_chunk(forward)
-
-    store_below = pltpu.make_async_copy(prefix_in, below, local_sem.at[1])
-    store_below.start()
+        each(pieces, forward)
 
     def drain(c):
         for side in (0, 1):
@@ -241,72 +237,90 @@
             def _():
                 row_copy(STEPS - 1, side, c).wait_send()
 
-        @pl.when(has["rows"][1])
-        def _():
-            prefix_copy(c).wait_send()
-
-    each_chunk(drain)
+    each(chunks, drain)
+
+    @pl.when(has["rows"][1])
+    def _():
+        each(pieces, lambda c: prefix_copy(c).wait_send())
+
     for side in (0, 1):
         for axis, copy in (("cols", col_copy), ("slabs", slab_copy)):
             @pl.when(has[axis][side])
             def _():
                 copy(STEPS - 1, side).wait_send()
+
+
+def finish(count, block, end, below, column_sum, tracer_end, running_sum, sems):
+    depth, width = end.shape[:2]
+    blocks = width // block
+    store_end = pltpu.make_async_copy(end, tracer_end, sems.at[blocks])
+    store_end.start()
+
+    def store_sum(b):
+        lines = pl.ds(b * block, block)
+        return pltpu.make_async_copy(running_sum.at[:, lines], column_sum.at[:, lines], sems.at[b])
+
+    def turn(b, carry):
+        def line(i, carry):
+            x = b * block + i
+            running = below[x]
+            for plane in range(depth):
+                running = running + end[plane, x]
+                running_sum[plane, x] = running / count
+            return carry
+
+        lax.fori_loop(0, block, line, 0)
+        store_sum(b).start()
+        return carry
+
+    lax.fori_loop(0, blocks, turn, 0)
     store_end.wait()
-    store_below.wait()
-
-
-def finish(count, end, below, column_sum, tracer_end):
-    running = below[...]
-    for plane in range(end.shape[0]):
-        value = end[plane]
-        running = running + value
-        tracer_end[plane] = value
-        column_sum[plane] = running / count
+    lax.fori_loop(0, blocks, lambda b, carry: (store_sum(b).wait(), carry)[1], 0)
 
 
 def body(sizes, tracer, crowding):
     depth, width, length, levels = tracer.shape
     kind = tracer.dtype
     chunk = math.gcd(width, CHUNK)
-    chunks = width // chunk
+    piece = math.gcd(chunk, PIECE)
+    chunks, pieces = width // chunk, width // piece
     anywhere = pl.BlockSpec(memory_space=pl.ANY)
+    held = pl.BlockSpec(memory_space=pltpu.VMEM)
     dma = pltpu.SemaphoreType.DMA
     end, below = pl.pallas_call(
-        functools.partial(evolve, sizes, chunk),
+        functools.partial(evolve, sizes, chunk, piece),
         out_shape=(
-            jax.ShapeDtypeStruct(tracer.shape, kind),
-            jax.ShapeDtypeStruct(tracer.shape[1:], kind),
+            pltpu.VMEM(tracer.shape, kind),
+            pltpu.VMEM(tracer.shape[1:], kind),
         ),
         in_specs=[anywhere, anywhere],
-        out_specs=(anywhere, anywhere),
+        out_specs=(held, held),
         scratch_shapes=[
             pltpu.VMEM((2, depth + 2, width + 2, length, levels), kind),
             pltpu.VMEM(tracer.shape, kind),
             pltpu.VMEM((2, 2, depth, width, levels), kind),
             pltpu.VMEM((2, 2, depth, width, levels), kind),
             pltpu.VMEM(tracer.shape[1:], kind),
-            pltpu.VMEM(tracer.shape[1:], kind),
             dma((2, 2, chunks)), dma((2, 2, chunks)),
             dma((2, 2)), dma((2, 2)),
             dma((2, 2)), dma((2, 2)),
-            dma((chunks,)), dma((chunks,)),
+            dma((pieces,)), dma((pieces,)),
             dma((2,)),
         ],
         compiler_params=pltpu.CompilerParams(
-            collective_id=0, has_side_effects=True, vmem_limit_bytes=60 * 1024 * 1024
+            collective_id=0, has_side_effects=True, vmem_limit_bytes=50 * 1024 * 1024
         ),
         name="evolve",
     )(tracer, crowding)
 
     block = math.gcd(width, 8)
-    whole = pl.BlockSpec((depth, block, length, levels), lambda i: (0, i, 0, 0))
-    plane = pl.BlockSpec((block, length, levels), lambda i: (i, 0, 0))
     return pl.pallas_call(
-        functools.partial(finish, depth * sizes["rows"]),
-        grid=(width // block,),
+        functools.partial(finish, depth * sizes["rows"], block),
         out_shape=(jax.ShapeDtypeStruct(tracer.shape, kind),) * 2,
-        in_specs=[whole, plane],
-        out_specs=(whole, whole),
+        in_specs=[held, held],
+        out_specs=(pl.BlockSpec(memory_space=pltpu.HBM),) * 2,
+        scratch_shapes=[pltpu.VMEM(tracer.shape, kind), dma((width // block + 1,))],
+        compiler_params=pltpu.CompilerParams(vmem_limit_bytes=16 * 1024 * 1024),
         name="finish",
     )(end, below)
 

time: 251 us -> 242 us (0.964)
  Pallas kernels: 250 us -> 241 us
    pallas_call x2, Pallas kernels: 250 us -> 241 us  [the longest x1 235 us: body(): pl.pallas_call(functools.partial(evolve, sizes, chunk, piece), out_shape=...]
where the time goes in v2:
time: 242 us
  Pallas kernels  241 us (100%)
    pallas_call x1, Pallas kernels, body(): pl.pallas_call(functools.partial(evolve, sizes, chunk, piece), out_shape=...  235 us
    pallas_call x1, Pallas kernels, body(): pl.pallas_call(functools.partial(finish, depth * sizes['rows'], block), o...  6.02 us

profile of v2, /device:TPU:24, one launch (start us, length us, event | category | flops | bytes accessed | tf_op | source)
XLA Modules:
  0.0 241.9 jit_solution(7215383711852292849)
XLA Ops:
  0.6 235.3 %evolve.1 = (f32[4,64,64,128]{3,2,1,0:T(8,128)S(1)}, f32[64,64,128]{2,1,0:T(8,128)S(1)}) custom-call(f32[4,64,64,128]{3,2,1,0:T(8,128)} %tracer.1, f32[4,64,64,128]{3,2,1,0:T(8,128)} %crowding.1), custom_call_target="tpu_custom_call" | custom-call | tf_op jit(solution)/shard_map/evolve/pallas_call | solution.py:290
  235.9 6.0 %finish.1 = (f32[4,64,64,128]{3,2,1,0:T(8,128)}, f32[4,64,64,128]{3,2,1,0:T(8,128)}) custom-call(f32[4,64,64,128]{3,2,1,0:T(8,128)S(1)} %get-tuple-element.4.end, f32[64,64,128]{2,1,0:T(8,128)S(1)} %get-tuple-element.5.below), custom_call_target="tpu_custom_call" | custom-call | tf_op jit(solution)/shard_map/finish/pallas_call | solution.py:317

commit v3 on v2

--- a/solution.py
+++ b/solution.py
@@ -10,17 +10,17 @@
 
 STEPS = 4
 CHUNK = 4
-PIECE = 1
+PARTS = 2
 MESH = pl.DeviceIdType.MESH
 
 
 def evolve(
-    sizes, chunk, piece, tracer, crowding, end, below,
-    field, crowd, edge_out, edge_in, prefix_out,
+    sizes, chunk, parts, tracer, crowding, end, column_sum,
+    field, crowd, edge_out, edge_in, below, prefix_out,
     row_send, row_recv, col_send, col_recv, slab_send, slab_recv, pre_send, pre_recv, local_sem,
 ):
     depth, width, length, _ = tracer.shape
-    chunks, pieces = width // chunk, width // piece
+    chunks, pieces = width // chunk, width * parts
     place = {axis: lax.axis_index(axis) for axis in sizes}
     has = {axis: (place[axis] > 0, place[axis] < sizes[axis] - 1) for axis in sizes}
 
@@ -65,8 +65,12 @@
             device_id=other("slabs", side), device_id_type=MESH,
         )
 
+    def piece_of(c):
+        part = length // parts
+        return c // parts, pl.ds(pl.multiple_of((c % parts) * part, part), part)
+
     def prefix_copy(c):
-        inner = pl.ds(c * piece, piece)
+        inner = piece_of(c)
         return pltpu.make_async_remote_copy(
             prefix_out.at[inner], below.at[inner], pre_send.at[c], pre_recv.at[c],
             device_id=other("rows", 1), device_id_type=MESH,
@@ -75,7 +79,6 @@
     load_field = pltpu.make_async_copy(tracer, field.at[0, pl.ds(1, depth), pl.ds(1, width)], local_sem.at[0])
     load_crowd = pltpu.make_async_copy(crowding, crowd, local_sem.at[1])
     load_field.start()
-    load_crowd.start()
 
     barrier = pltpu.get_barrier_semaphore()
     greeted = 0
@@ -99,6 +102,7 @@
                 row_copy(0, side, c).start()
 
     each(chunks, start_rows)
+    load_crowd.start()
     for side in (0, 1):
         @pl.when(has["cols"][side])
         def _():
@@ -203,8 +207,8 @@
             if last:
                 @pl.when(jnp.logical_and(jnp.logical_not(has["rows"][0]), has["rows"][1]))
                 def _():
-                    for k in range(chunk // piece):
-                        prefix_copy(c * (chunk // piece) + k).start()
+                    for k in range(chunk * parts):
+                        prefix_copy(c * (chunk * parts) + k).start()
             else:
                 for side in (0, 1):
                     @pl.when(has["rows"][side])
@@ -219,79 +223,72 @@
                     def _():
                         copy(step + 1, side).start()
 
-    @pl.when(has["rows"][0])
-    def _():
-        def forward(c):
-            prefix_copy(c).wait_recv()
-
-            @pl.when(has["rows"][1])
-            def _():
-                inner = pl.ds(c * piece, piece)
-                prefix_out[inner] = prefix_out[inner] + below[inner]
-                prefix_copy(c).start()
-        each(pieces, forward)
-
-    def drain(c):
-        for side in (0, 1):
-            @pl.when(has["rows"][side])
-            def _():
-                row_copy(STEPS - 1, side, c).wait_send()
-
-    each(chunks, drain)
-
-    @pl.when(has["rows"][1])
-    def _():
-        each(pieces, lambda c: prefix_copy(c).wait_send())
-
+    def drain(side):
+        @pl.when(has["rows"][side])
+        def _():
+            each(chunks, lambda c: row_copy(STEPS - 1, side, c).wait_send())
+
+    drain(0)
     for side in (0, 1):
         for axis, copy in (("cols", col_copy), ("slabs", slab_copy)):
             @pl.when(has[axis][side])
             def _():
                 copy(STEPS - 1, side).wait_send()
 
-
-def finish(count, block, end, below, column_sum, tracer_end, running_sum, sems):
-    depth, width = end.shape[:2]
-    blocks = width // block
-    store_end = pltpu.make_async_copy(end, tracer_end, sems.at[blocks])
-    store_end.start()
-
-    def store_sum(b):
-        lines = pl.ds(b * block, block)
-        return pltpu.make_async_copy(running_sum.at[:, lines], column_sum.at[:, lines], sems.at[b])
-
-    def turn(b, carry):
-        def line(i, carry):
-            x = b * block + i
-            running = below[x]
-            for plane in range(depth):
-                running = running + end[plane, x]
-                running_sum[plane, x] = running / count
-            return carry
-
-        lax.fori_loop(0, block, line, 0)
-        store_sum(b).start()
-        return carry
-
-    lax.fori_loop(0, blocks, turn, 0)
-    store_end.wait()
-    lax.fori_loop(0, blocks, lambda b, carry: (store_sum(b).wait(), carry)[1], 0)
+    share = 1.0 / (depth * sizes["rows"])
+
+    def forward(c):
+        x, part = piece_of(c)
+
+        @pl.when(has["rows"][0])
+        def _():
+            prefix_copy(c).wait_recv()
+
+            @pl.when(has["rows"][1])
+            def _():
+                prefix_out[x, part] = prefix_out[x, part] + below[x, part]
+                prefix_copy(c).start()
+
+        running = below[x, part]
+        for plane in range(depth):
+            running = running + end[plane, x, part]
+            column_sum[plane, x, part] = running * share
+
+    each(pieces, forward)
+    drain(1)
+
+    @pl.when(has["rows"][1])
+    def _():
+        each(pieces, lambda c: prefix_copy(c).wait_send())
+
+
+def finish(*refs):
+    held, placed, sems = refs[:2], refs[2:4], refs[4]
+    depth = held[0].shape[0]
+    copies = [
+        pltpu.make_async_copy(held[k].at[plane], placed[k].at[plane], sems.at[k, plane])
+        for k in range(2) for plane in range(depth)
+    ]
+    for copy in copies:
+        copy.start()
+    for copy in copies:
+        copy.wait()
 
 
 def body(sizes, tracer, crowding):
     depth, width, length, levels = tracer.shape
     kind = tracer.dtype
     chunk = math.gcd(width, CHUNK)
-    piece = math.gcd(chunk, PIECE)
-    chunks, pieces = width // chunk, width // piece
+    parts = PARTS if length % (8 * PARTS) == 0 else 1
+    chunks, pieces = width // chunk, width * parts
     anywhere = pl.BlockSpec(memory_space=pl.ANY)
     held = pl.BlockSpec(memory_space=pltpu.VMEM)
     dma = pltpu.SemaphoreType.DMA
-    end, below = pl.pallas_call(
-        functools.partial(evolve, sizes, chunk, piece),
+    end, column_sum = pl.pallas_call(
+        functools.partial(evolve, sizes, chunk, parts),
         out_shape=(
             pltpu.VMEM(tracer.shape, kind),
-            pltpu.VMEM(tracer.shape[1:], kind),
+            pltpu.VMEM(tracer.shape, kind),
         ),
         in_specs=[anywhere, anywhere],
         out_specs=(held, held),
@@ -301,6 +298,7 @@
             pltpu.VMEM((2, 2, depth, width, levels), kind),
             pltpu.VMEM((2, 2, depth, width, levels), kind),
             pltpu.VMEM(tracer.shape[1:], kind),
+            pltpu.VMEM(tracer.shape[1:], kind),
             dma((2, 2, chunks)), dma((2, 2, chunks)),
             dma((2, 2)), dma((2, 2)),
             dma((2, 2)), dma((2, 2)),
@@ -308,21 +306,20 @@
             dma((2,)),
         ],
         compiler_params=pltpu.CompilerParams(
-            collective_id=0, has_side_effects=True, vmem_limit_bytes=50 * 1024 * 1024
+            collective_id=0, has_side_effects=True, vmem_limit_bytes=42 * 1024 * 1024
         ),
         name="evolve",
     )(tracer, crowding)
 
-    block = math.gcd(width, 8)
     return pl.pallas_call(
-        functools.partial(finish, depth * sizes["rows"], block),
+        finish,
         out_shape=(jax.ShapeDtypeStruct(tracer.shape, kind),) * 2,
         in_specs=[held, held],
         out_specs=(pl.BlockSpec(memory_space=pltpu.HBM),) * 2,
-        scratch_shapes=[pltpu.VMEM(tracer.shape, kind), dma((width // block + 1,))],
-        compiler_params=pltpu.CompilerParams(vmem_limit_bytes=16 * 1024 * 1024),
+        scratch_shapes=[dma((2, depth))],
+        compiler_params=pltpu.CompilerParams(vmem_limit_bytes=1024 * 1024),
         name="finish",
-    )(end, below)
+    )(column_sum, end)
 
 
 def solution(mesh):

time: 242 us -> 243 us (level)
  no operation moved by 1% of the time
where the time goes in v3:
time: 243 us
  Pallas kernels  242 us (100%)
    pallas_call x1, Pallas kernels, body(): pl.pallas_call(functools.partial(evolve, sizes, chunk, parts), out_shape=...  236 us
    pallas_call x1, Pallas kernels, body(): pl.pallas_call(finish, out_shape=(jax.ShapeDtypeStruct(tracer.shape, kind...  5.93 us

profile of v3, /device:TPU:24, one launch (start us, length us, event | category | flops | bytes accessed | tf_op | source)
XLA Modules:
  0.0 242.7 jit_solution(8343945326548574873)
XLA Ops:
  0.6 236.1 %evolve.1 = (f32[4,64,64,128]{3,2,1,0:T(8,128)S(1)}, f32[4,64,64,128]{3,2,1,0:T(8,128)S(1)}) custom-call(f32[4,64,64,128]{3,2,1,0:T(8,128)} %tracer.1, f32[4,64,64,128]{3,2,1,0:T(8,128)} %crowding.1), custom_call_target="tpu_custom_call" | custom-call | tf_op jit(solution)/shard_map/evolve/pallas_call | solution.py:287
  236.8 5.9 %finish.1 = (f32[4,64,64,128]{3,2,1,0:T(8,128)}, f32[4,64,64,128]{3,2,1,0:T(8,128)}) custom-call(f32[4,64,64,128]{3,2,1,0:T(8,128)S(1)} %get-tuple-element.4.refs_0_, f32[4,64,64,128]{3,2,1,0:T(8,128)S(1)} %get-tuple-element.5.refs_1_), custom_call_target="tpu_custom_call" | custom-call | tf_op jit(solution)/shard_map/finish/pallas_call | solution.py:314

commit v4 on v3

--- a/solution.py
+++ b/solution.py
@@ -9,8 +9,8 @@
 from jax.sharding import PartitionSpec as P
 
 STEPS = 4
-CHUNK = 4
-PARTS = 2
+CHUNK = 8
+PARTS = 1
 MESH = pl.DeviceIdType.MESH
 
 

time: 243 us -> 242 us (level)
  no operation moved by 1% of the time
where the time goes in v4:
time: 242 us; the launch traced here: 241 us
  Pallas kernels  241 us (100%)
    pallas_call x1, Pallas kernels, body(): pl.pallas_call(functools.partial(evolve, sizes, chunk, parts), out_shape=...  235 us
    pallas_call x1, Pallas kernels, body(): pl.pallas_call(finish, out_shape=(jax.ShapeDtypeStruct(tracer.shape, kind...  5.93 us

profile of v4, /device:TPU:24, one launch (start us, length us, event | category | flops | bytes accessed | tf_op | source)
XLA Modules:
  0.0 241.5 jit_solution(15341202924729510838)
XLA Ops:
  0.6 234.9 %evolve.1 = (f32[4,64,64,128]{3,2,1,0:T(8,128)S(1)}, f32[4,64,64,128]{3,2,1,0:T(8,128)S(1)}) custom-call(f32[4,64,64,128]{3,2,1,0:T(8,128)} %tracer.1, f32[4,64,64,128]{3,2,1,0:T(8,128)} %crowding.1), custom_call_target="tpu_custom_call" | custom-call | tf_op jit(solution)/shard_map/evolve/pallas_call | solution.py:287
  235.5 5.9 %finish.1 = (f32[4,64,64,128]{3,2,1,0:T(8,128)}, f32[4,64,64,128]{3,2,1,0:T(8,128)}) custom-call(f32[4,64,64,128]{3,2,1,0:T(8,128)S(1)} %get-tuple-element.4.refs_0_, f32[4,64,64,128]{3,2,1,0:T(8,128)S(1)} %get-tuple-element.5.refs_1_), custom_call_target="tpu_custom_call" | custom-call | tf_op jit(solution)/shard_map/finish/pallas_call | solution.py:314
